TPU v7x, 64 devices: a 2x2x8 block of a 4x4x8 slice. The times are simulated.
64 devices in a mesh: dp: 4 (over x, y), sp: 16 (over z, core).
Axes of the slice: x: 2, y: 2, z: 8, core: 2. Of those that a mesh axis runs over, the one named last changes fastest.
The devices are a block of a 4x4x8 slice.
Arguments:
- q: bfloat16 [128, 64, 128], P('dp'), parts along dimension 0
- k: bfloat16 [128, 8192, 8, 128], P('dp', 'sp'), parts along dimension 0
- v: bfloat16 [128, 8192, 8, 128], P('dp', 'sp'), parts along dimension 0
Outputs:
- q: bfloat16 [128, 64, 128], P('dp'), parts along dimension 0
There are 4 independent parts. A program takes and returns all parts, laid end to end along the dimension named above; each array names one.
All inputs are finite; a program needn't handle non-finite values.
Results may differ from a plain program's by a relative error of at most 0.012.
Values are sent between devices in bfloat16 or wider.
A program may use at most 768 MiB of HBM per device.

v0:
```python
import jax
import jax.numpy as jnp
from jax import lax
from jax.sharding import PartitionSpec as P


def einsum(form, a, b):
    return jnp.einsum(form, a.astype(jnp.float32), b.astype(jnp.float32))


def part_of(q, k, v):
    grouped = q.reshape(q.shape[0], k.shape[2], -1, q.shape[2])
    scores = einsum("bgsd,bugd->bgsu", grouped, k) * q.shape[2] ** -0.5
    high = jnp.max(scores, -1, keepdims=True)
    weights = jnp.exp(scores - high)
    seen = einsum("bgsu,bugd->bgsd", weights.astype(jnp.bfloat16), v)
    return jnp.concatenate([seen, jnp.sum(weights, -1, keepdims=True), high], -1)


def together(parts):
    seen, total, high = parts[..., :-2], parts[..., -2:-1], parts[..., -1:]
    scale = jnp.exp(high - jnp.max(high, 0))
    return (jnp.sum(seen * scale, 0) / jnp.sum(total * scale, 0)).astype(jnp.bfloat16)


def solution(mesh):
    def step(q, k, v):
        return together(lax.all_gather(part_of(q, k, v), "sp")).reshape(q.shape)

    return jax.shard_map(
        step,
        mesh=mesh,
        in_specs=(P("dp", None, None), P("dp", "sp", None, None), P("dp", "sp", None, None)),
        out_specs=P("dp", None, None),
        check_vma=False,
    )
```

profile of v0, /device:TPU:21, one launch (start us, length us, event | category | flops | bytes accessed | tf_op | source)
XLA Modules:
  0.0 297.7 jit_solution(15889040606131357668)
XLA Ops:
  6.5 0.0 copy-start
  6.6 0.0 all-gather.3.cloned.1.call-start
  6.6 1.0 copy-done
  7.6 14.7 %multiply_reduce_fusion = (f32[32,8,8]{2,1,0:T(8,128)S(1)}, f32[32,8,8,512]{3,2,1,0:T(8,128)S(1)}) fusion(bf16[32,512,8,128]{3,2,1,0:T(8,128)(2,1)} %param.4, bf16[32,64,128]{2,1,0:T(8,128)(2,1)S(1)} %copy-done), kind=kOutput, calls=%fused_computation.11 | convolution fusion | flops 270530560 | bytes 38281216 | tf_op jit(solution)/shard_map/bgsd,bugd->bgsu/dot_general | solution.py:8
  22.3 0.0 copy-start.2
  22.3 1.9 copy-done.2
  24.3 1.3 fusion.6
  25.6 16.4 %fusion = f32[32,8,8,128]{3,2,1,0:T(8,128)S(1)} fusion(bf16[32,512,8,128]{3,2,1,0:T(8,128)(2,1)} %param.5, f32[32,8,8,512]{3,2,1,0:T(8,128)} %copy-done.2, f32[32,8,8]{2,1,0:T(8,128)S(1)} %get-tuple-element.7), kind=kOutput, calls=%fused_computation | convolution fusion | flops 271581184 | bytes 38805504 | tf_op jit(solution)/shard_map/bgsu,bugd->bgsd/dot_general | solution.py:8
  42.0 1.6 copy.35
  43.5 2.5 copy.36
  46.1 2.9 pad_maximum_fusion
  49.0 0.1 all-gather.3.cloned.1.call-update
  49.1 176.2 %all-gather.3.cloned.1.call-done = f32[512,8,8,130]{3,2,1,0:T(8,128)} async-done(((f32[32,8,8,130]{3,2,1,0:T(8,128)}), f32[512,8,8,130]{3,2,1,0:T(8,128)}) %all-gather.3.cloned.1.call-update) | async-done | bytes 17039376 | tf_op jit(solution)/shard_map/all_gather | solution.py:28
  225.3 10.4 %slice_reduce_fusion = f32[32,8,8]{2,1,0:T(8,128)S(1)} fusion(f32[16,32,8,8,130]{4,3,2,1,0:T(8,128)} %bitcast.15), kind=kLoop, calls=%fused_computation.9 | loop fusion | flops 30720 | bytes 139264 | tf_op jit(solution)/shard_map/reduce_max | solution.py:22
  235.8 17.4 %fusion.4 = (f32[32,8,8]{2,1,0:T(8,128)S(1)}, f32[16,32,8,8,1]{4,3,2,1,0:T(8,128)}) fusion(f32[16,32,8,8,130]{4,3,2,1,0:T(8,128)} %bitcast.16, f32[32,8,8]{2,1,0:T(8,128)S(1)} %slice_reduce_fusion), kind=kLoop, calls=%fused_computation.5 | loop fusion | flops 96256 | bytes 409600 | tf_op jit(solution)/shard_map/reduce_sum | solution.py:23
  253.1 0.1 copy.39
  253.2 0.1 copy.40
  253.3 28.6 %copy.45 = f32[16,32,8,8,1]{3,2,1,0,4:T(8,128)S(1)} copy(f32[16,32,8,8,1]{4,3,2,1,0:T(8,128)} %get-tuple-element.6) | data formatting | bytes 262144 | tf_op jit(solution)/shard_map/mul | solution.py:23
  281.9 0.0 copy-start.1
  281.9 7.8 %fusion.5 = f32[32,8,8,128]{3,2,1,0:T(8,128)S(1)} fusion(f32[16,32,8,8,130]{4,3,2,1,0:T(8,128)} %bitcast.17, f32[16,32,8,8]{3,2,1,0:T(8,128)S(1)} %bitcast.18), kind=kLoop, calls=%fused_computation.7 | loop fusion | flops 8126464 | bytes 17956864 | tf_op jit(solution)/shard_map/reduce_sum | solution.py:23
  289.7 1.1 fusion.11
  290.8 0.0 copy-done.1
Async XLA Ops:
  6.5 1.0 copy-start
  6.6 218.7 %all-gather.3.cloned.1.call-start = ((), (), s32[]{:S(2)}) async-start(), calls=%async_computation | async-start | bytes 35651584 | tf_op jit(solution)/shard_map/all_gather | solution.py:28
  22.3 1.9 copy-start.2
  281.9 9.0 %copy-start.1 = (bf16[32,64,128]{2,1,0:T(8,128)(2,1)S(1)}, bf16[32,64,128]{2,1,0:T(8,128)(2,1)}, u32[]{:S(2)}) copy-start(bf16[32,64,128]{2,1,0:T(8,128)(2,1)} %param.3) | copy-start | bytes 1572868
Sparse Core Ops, SparseCore 0:
  49.2 176.0 all-gather.2
where the time goes:
time: 298 us
  waiting for transfers between devices  176 us (59%)
  other arithmetic  41 us (14%)
  local copies, waits for them, and re-layouts  35.8 us (12%)
  matrix products  31.1 us (10%)
  between operations  13.5 us (5%)
    all_gather x1, waiting for transfers between devices, step(): return together(lax.all_gather(part_of(q, k, v), 'sp')).reshape(q.shape)  176 us
    dot_general x2, matrix products, einsum(): return jnp.einsum(form, a.astype(jnp.float32), b.astype(jnp.float32))  31.1 us
    mul x1, local copies, waits for them, and re-layouts, together(): seen * scale  28.6 us
    reduce_sum x1, other arithmetic, together(): jnp.sum(total * scale, 0)  17.4 us
    reduce_max x1, other arithmetic, together(): scale = jnp.exp(high - jnp.max(high, 0))  10.4 us
    reduce_sum x1, other arithmetic, together(): jnp.sum(seen * scale, 0) / jnp.sum(total * scale, 0)  7.8 us
  transfers between devices with their start and end apart: 1, of which 1 were waited for; matrix products, arithmetic and copies ran while one was open for 0% of the time, Pallas kernels for 0%

commit v1 on v0

v1 whole, which is shorter than its diff:
```python
import functools

import jax
import jax.numpy as jnp
from jax import lax
from jax.experimental import pallas as pl
from jax.experimental.pallas import tpu as pltpu
from jax.sharding import PartitionSpec as P

SLOTS = 8
BLOCK = 512
CORES = 2
SUB = 8
LOG2E = 1.4426950408889634


def chunks_of(n, unit):
    sizes = [4 * unit] * (n // (4 * unit) - 1) + [2 * unit, unit, unit]
    assert sum(sizes) == n
    return [(sum(sizes[:i]), g) for i, g in enumerate(sizes)]


def kernel(size, chunks, scale, heads, q_ref, k_hbm, v_hbm, o_ref, kbuf, vbuf, sbuf, pbuf, send, stat, cols, *rest):
    nc = len(chunks)
    recv, rstat = rest[:nc], rest[nc : 2 * nc]
    ksem, vsem, sems = rest[2 * nc :]
    PART_OUT, PART_IN, STAT_OUT, STAT_IN, RES_OUT, RES_IN, PASS_OUT, PASS_IN = range(8)
    n, nq, d = q_ref.shape
    rows = k_hbm.shape[1]
    half = rows // 2
    nblk = half // BLOCK
    per = nq // SUB
    c2 = scale * LOG2E
    me = lax.axis_index("sp")
    zs = size // CORES
    core, z = lax.rem(me, CORES), me // CORES

    def owner(j):
        return lax.rem(j, CORES) * zs + j // CORES

    barrier = pltpu.get_barrier_semaphore()
    for i in range(1, size):
        pl.semaphore_signal(barrier, inc=1, device_id={"sp": lax.rem(me + i, size)}, device_id_type=pl.DeviceIdType.MESH)

    def kcopy(s):
        return pltpu.make_async_copy(k_hbm.at[s], kbuf.at[lax.rem(s, SLOTS)], ksem.at[lax.rem(s, SLOTS)])

    def vcopy(s):
        return pltpu.make_async_copy(v_hbm.at[s], vbuf.at[lax.rem(s, SLOTS)], vsem.at[lax.rem(s, SLOTS)])

    for s in range(SLOTS):
        kcopy(s).start()
        vcopy(s).start()

    row = lax.broadcasted_iota(jnp.int32, (heads, 2 * nq), 0)
    lane = lax.broadcasted_iota(jnp.int32, (heads, 2 * nq), 1)
    keep = row == lax.rem(lane, nq) // (nq // heads)
    first = lax.broadcasted_iota(jnp.int32, (1, 2 * nq), 1) < nq

    def scores(s, b, w, m):
        slot = lax.rem(s, SLOTS)
        k0 = kbuf[slot, pl.ds(b * BLOCK, BLOCK), :]
        k1 = kbuf[slot, pl.ds(half + b * BLOCK, BLOCK), :]
        x = lax.dot_general(jnp.concatenate([k0, k1], 1), w, (((1,), (1,)), ((), ())), preferred_element_type=jnp.float32)
        x = jnp.where(keep[None], x.reshape(BLOCK // heads, heads, 2 * nq), -jnp.inf)
        sbuf[pl.ds(b * BLOCK, BLOCK), :] = x.reshape(BLOCK, 2 * nq)
        return jnp.maximum(m, jnp.max(x, 0))

    def weights(b, mc, l):
        p = jnp.exp2(sbuf[pl.ds(b * BLOCK, BLOCK), :] * c2 - mc)
        pbuf[:, pl.ds(b * BLOCK, BLOCK)] = p.astype(jnp.bfloat16).T
        return l + jnp.sum(p.reshape(BLOCK // heads, heads, 2 * nq), 0)

    def values(s, b, acc):
        slot = lax.rem(s, SLOTS)
        at = pl.ds(b * BLOCK, BLOCK)
        acc = acc + jnp.dot(pbuf[:nq, at], vbuf[slot, at, :], preferred_element_type=jnp.float32)
        return acc + jnp.dot(pbuf[nq:, at], vbuf[slot, pl.ds(half + b * BLOCK, BLOCK), :], preferred_element_type=jnp.float32)

    def fold(x, op, reduce):
        x = reduce(x, 0, keepdims=True)
        return op(x, pltpu.roll(x, nq, 1))

    def stage(s, state, which):
        m8, l8, m2 = state
        m = jnp.full((heads, 2 * nq), -jnp.inf, jnp.float32)
        l = jnp.zeros((heads, 2 * nq), jnp.float32)
        acc = jnp.zeros((nq, d), jnp.float32)
        if "A" in which:
            q = q_ref[s]
            zero = jnp.zeros_like(q)
            w = jnp.concatenate([jnp.concatenate([q, zero], 1), jnp.concatenate([zero, q], 1)], 0)
        m1 = fold(m8, jnp.maximum, jnp.max)
        for b in range(nblk):
            if "C" in which:
                acc = values(s - 2, b, acc)
            if "B" in which:
                l = weights(b, m1 * c2, l)
            if "A" in which:
                m = scores(s, b, w, m)
        if "C" in which:
            send[pl.ds((s - 2) * per, per)] = acc.reshape(per, SUB, d).astype(send.dtype)
            stat[s - 2] = jnp.where(first, m2, fold(l8, jnp.add, jnp.sum))
        return m, l, m1

    def shape_of(c):
        base, g = chunks[c]
        r = g * per // size
        return base, g, r

    def rows_of(c, o):
        base, _, r = shape_of(c)
        return pl.ds(base * per + o * r, r)

    def seq_of(c, o):
        base, _, r = shape_of(c)
        return base + (o * r) // per

    def remote(src, dst, out, into, j):
        return pltpu.make_async_remote_copy(src, dst, out, into, device_id={"sp": j}, device_id_type=pl.DeviceIdType.MESH)

    def wait_for(ref, sem):
        pltpu.make_async_copy(ref, ref, sem).wait()

    def send_parts(c):
        for i in range(1, size):
            j = lax.rem(me + i, size)
            o = owner(j)
            remote(send.at[rows_of(c, o)], recv[c].at[me], sems.at[PART_OUT, c], sems.at[PART_IN, c], j).start()
            remote(stat.at[seq_of(c, o)], rstat[c].at[me], sems.at[STAT_OUT, c], sems.at[STAT_IN, c], j).start()

    def combine(c, direct):
        base, g, r = shape_of(c)
        o = owner(me)
        recv[c][me] = send[rows_of(c, o)]
        rstat[c][me] = stat[seq_of(c, o)]
        wait_for(rstat[c].at[pl.ds(0, size - 1)], sems.at[STAT_IN, c])
        wait_for(recv[c].at[pl.ds(0, size - 1)], sems.at[PART_IN, c])
        st = rstat[c][...].reshape(size, 2 * nq)
        e = jnp.exp2((st - jnp.max(st, 0, keepdims=True)) * c2)
        f = e / jnp.sum(e * pltpu.roll(st, nq, 1), 0, keepdims=True)
        cols[...] = f.T
        f = cols[pl.ds(pl.multiple_of(lax.rem(o * r, per) * SUB, SUB), r * SUB), :]
        acc = jnp.zeros((r * SUB, d), jnp.float32)
        for j in range(size):
            acc = acc + recv[c][j].astype(jnp.float32).reshape(r * SUB, d) * f[:, j : j + 1]
        mine = rows_of(c, o)
        o_ref[mine] = acc.reshape(r, SUB, d).astype(o_ref.dtype)
        if direct:
            peers = [lax.rem(me + i, size) for i in range(1, size)]
        else:
            peers = [lax.rem(z + i, zs) * CORES + core for i in range(1, zs)]
        for j in peers:
            remote(o_ref.at[mine], o_ref.at[mine], sems.at[RES_OUT, c], sems.at[RES_IN, c], j).start()

    def count(c, k):
        return o_ref.at[pl.ds(0, k * shape_of(c)[2])]

    def pass_on(c):
        base, g, r = shape_of(c)
        wait_for(count(c, zs - 1), sems.at[RES_IN, c])
        own = o_ref.at[pl.ds(base * per + core * zs * r, zs * r)]
        remote(own, own, sems.at[PASS_OUT, c], sems.at[PASS_IN, c], z * CORES + lax.rem(core + 1, CORES)).start()

    last = nc - 1
    ends = [base + g for base, g in chunks]
    events = {}
    for c in range(nc):
        events.setdefault(ends[c], []).append(functools.partial(send_parts, c))
    late = []
    for c in range(last):
        at = ends[c] + chunks[c][1] + chunks[c][1] // 2
        if at < n - 1:
            events.setdefault(at, []).append(functools.partial(combine, c, False))
        else:
            late.append(c)
    early = [c for c in range(last) if c not in late]

    state = (jnp.zeros((heads, 2 * nq), jnp.float32), jnp.zeros((heads, 2 * nq), jnp.float32), jnp.zeros((1, 2 * nq), jnp.float32))

    def refill(copy, s):
        @pl.when(s + SLOTS < n)
        def _():
            copy(s + SLOTS).start()

    kcopy(0).wait()
    state = stage(0, state, "A")
    refill(kcopy, 0)
    kcopy(1).wait()
    state = stage(1, state, "BA")
    refill(kcopy, 1)

    def body(s, state):
        kcopy(s).wait()
        vcopy(s - 2).wait()
        state = stage(s, state, "ABC")
        refill(kcopy, s)
        refill(vcopy, s - 2)
        return state

    at = 2
    waited = False
    for e in sorted(x for x in events if x <= n - 2) + [n - 2]:
        if e + 2 > at:
            state = lax.fori_loop(at, e + 2, body, state)
            at = e + 2
        if not waited:
            pl.semaphore_wait(barrier, size - 1)
            waited = True
        for run in events.pop(e, []):
            run()
    vcopy(n - 2).wait()
    state = stage(n, state, "BC")
    for run in events.pop(n - 1, []):
        run()
    vcopy(n - 1).wait()
    state = stage(n + 1, state, "C")
    for run in events.pop(n, []):
        run()
    for c in early:
        pass_on(c)
    for c in late:
        combine(c, False)
    combine(last, True)
    for c in late:
        pass_on(c)
    for c in range(last):
        base, g, r = shape_of(c)
        wait_for(count(c, zs), sems.at[PASS_IN, c])
    wait_for(count(last, size - 1), sems.at[RES_IN, last])
    for c in range(nc):
        wait_for(recv[c].at[pl.ds(0, size - 1)], sems.at[PART_OUT, c])
        wait_for(rstat[c].at[pl.ds(0, size - 1)], sems.at[STAT_OUT, c])
        wait_for(count(c, size - 1 if c == last else zs - 1), sems.at[RES_OUT, c])
        if c < last:
            wait_for(count(c, zs), sems.at[PASS_OUT, c])


def solution(mesh):
    size = mesh.shape["sp"]

    def step(q, k, v):
        n, nq, d = q.shape
        t, heads = k.shape[1:3]
        per = nq // SUB
        chunks = chunks_of(n, size // per)
        nc = len(chunks)
        rows = t * heads
        out = pl.pallas_call(
            functools.partial(kernel, size, chunks, d**-0.5, heads),
            out_shape=jax.ShapeDtypeStruct((n * per, SUB, d), q.dtype),
            in_specs=[pl.BlockSpec(memory_space=pltpu.VMEM), pl.BlockSpec(memory_space=pl.ANY), pl.BlockSpec(memory_space=pl.ANY)],
            out_specs=pl.BlockSpec(memory_space=pltpu.VMEM),
            scratch_shapes=[
                pltpu.VMEM((SLOTS, rows, d), k.dtype),
                pltpu.VMEM((SLOTS, rows, d), v.dtype),
                pltpu.VMEM((rows // 2, 2 * nq), jnp.float32),
                pltpu.VMEM((2 * nq, rows // 2), jnp.bfloat16),
                pltpu.VMEM((n * per, SUB, d), jnp.bfloat16),
                pltpu.VMEM((n, 1, 2 * nq), jnp.float32),
                pltpu.VMEM((2 * nq, size), jnp.float32),
                *[pltpu.VMEM((size, g * per // size, SUB, d), jnp.bfloat16) for _, g in chunks],
                *[pltpu.VMEM((size, 1, 2 * nq), jnp.float32) for _ in chunks],
                pltpu.SemaphoreType.DMA((SLOTS,)),
                pltpu.SemaphoreType.DMA((SLOTS,)),
                pltpu.SemaphoreType.DMA((8, nc)),
            ],
            compiler_params=pltpu.CompilerParams(collective_id=0, has_side_effects=True, vmem_limit_bytes=60 * 1024 * 1024),
        )(q, k.reshape(n, rows, d), v.reshape(n, rows, d))
        return out.reshape(q.shape)

    return jax.shard_map(
        step,
        mesh=mesh,
        in_specs=(P("dp", None, None), P("dp", "sp", None, None), P("dp", "sp", None, None)),
        out_specs=P("dp", None, None),
        check_vma=False,
    )
```

time: 298 us -> 48.7 us (0.16)
  waiting for transfers between devices: 176 us -> 0 us
  Pallas kernels: 0 us -> 46.7 us
  other arithmetic: 41 us -> 0 us
  local copies, waits for them, and re-layouts: 35.8 us -> 1.87 us
  matrix products: 31.1 us -> 0 us
  between operations: 13.5 us -> 0.01 us
    all_gather x1 -> x0, waiting for transfers between devices: 176 us -> none  [step(): return together(lax.all_gather(part_of(q, k, v), 'sp')).reshape(q.shape)]
    pallas_call x0 -> x1, Pallas kernels: none -> 46.7 us  [step(): pl.pallas_call(functools.partial(kernel, size, chunks, d ** (-0.5), heads...]
    dot_general x2 -> x0, matrix products: 31.1 us -> none  [einsum(): return jnp.einsum(form, a.astype(jnp.float32), b.astype(jnp.float32))]
    mul x1 -> x0, local copies, waits for them, and re-layouts: 28.6 us -> none  [together(): seen * scale]
    reduce_sum x3 -> x0, other arithmetic: 26.5 us -> none  [the longest x1 17.4 us: together(): jnp.sum(total * scale, 0)]
    reduce_max x1 -> x0, other arithmetic: 10.4 us -> none  [together(): scale = jnp.exp(high - jnp.max(high, 0))]
    broadcast_in_dim x2 -> x0, local copies, waits for them, and re-layouts: 4.1 us -> none  [the longest x1 2.55 us: part_of(): high = jnp.max(scores, -1, keepdims=True)]
  transfers between devices with their start and end apart: 1 -> 0, of which waited for: 1 -> 0; matrix products, arithmetic and copies ran while one was open for 0% -> 0% of each run, Pallas kernels for 0% -> 0%
where the time goes in v1:
time: 48.7 us; the launch traced here: 48.6 us
  Pallas kernels  46.7 us (96%)
  local copies, waits for them, and re-layouts  1.87 us (4%)
    pallas_call x1, Pallas kernels, step(): pl.pallas_call(functools.partial(kernel, size, chunks, d ** (-0.5), heads...  46.7 us
    unnamed x1, local copies, waits for them, and re-layouts  1.87 us

profile of v1, /device:TPU:21, one launch (start us, length us, event | category | flops | bytes accessed | tf_op | source)
XLA Modules:
  0.0 48.6 jit_solution(16700389310112144852)
XLA Ops:
  0.0 46.7 %shard_map.37 = bf16[256,8,128]{2,1,0:T(8,128)(2,1)} custom-call(bf16[32,64,128]{2,1,0:T(8,128)(2,1)} %q_ref.1, bf16[32,4096,128]{2,1,0:T(8,128)(2,1)} %bitcast.3, bf16[32,4096,128]{2,1,0:T(8,128)(2,1)} %bitcast.4), custom_call_target="tpu_custom_call" | custom-call | tf_op jit(solution)/shard_map/pallas_call | solution.py:249
  46.7 1.9 %copy.5 = bf16[32,64,128]{2,1,0:T(8,128)(2,1)} copy(bf16[32,64,128]{2,1,0:T(8,128)(2,1)} %bitcast.5) | data formatting | bytes 1048576

commit v2 on v1

--- a/solution.py
+++ b/solution.py
@@ -20,12 +20,13 @@
     return [(sum(sizes[:i]), g) for i, g in enumerate(sizes)]
 
 
-def kernel(size, chunks, scale, heads, q_ref, k_hbm, v_hbm, o_ref, kbuf, vbuf, sbuf, pbuf, send, stat, cols, *rest):
+def kernel(size, chunks, scale, heads, q_hbm, k_hbm, v_hbm, o_ref, q_ref, kbuf, vbuf, sb0, sb1, pb0, pb1, send, stat, cols, *rest):
     nc = len(chunks)
     recv, rstat = rest[:nc], rest[nc : 2 * nc]
-    ksem, vsem, sems = rest[2 * nc :]
+    qsem, ksem, vsem, sems = rest[2 * nc :]
+    sbufs, pbufs = (sb0, sb1), (pb0, pb1)
     PART_OUT, PART_IN, STAT_OUT, STAT_IN, RES_OUT, RES_IN, PASS_OUT, PASS_IN = range(8)
-    n, nq, d = q_ref.shape
+    n, nq, d = q_hbm.shape
     rows = k_hbm.shape[1]
     half = rows // 2
     nblk = half // BLOCK
@@ -48,6 +49,8 @@
     def vcopy(s):
         return pltpu.make_async_copy(v_hbm.at[s], vbuf.at[lax.rem(s, SLOTS)], vsem.at[lax.rem(s, SLOTS)])
 
+    qcopy = pltpu.make_async_copy(q_hbm, q_ref, qsem)
+    qcopy.start()
     for s in range(SLOTS):
         kcopy(s).start()
         vcopy(s).start()
@@ -57,7 +60,7 @@
     keep = row == lax.rem(lane, nq) // (nq // heads)
     first = lax.broadcasted_iota(jnp.int32, (1, 2 * nq), 1) < nq
 
-    def scores(s, b, w, m):
+    def scores(s, b, w, m, sbuf):
         slot = lax.rem(s, SLOTS)
         k0 = kbuf[slot, pl.ds(b * BLOCK, BLOCK), :]
         k1 = kbuf[slot, pl.ds(half + b * BLOCK, BLOCK), :]
@@ -66,12 +69,12 @@
         sbuf[pl.ds(b * BLOCK, BLOCK), :] = x.reshape(BLOCK, 2 * nq)
         return jnp.maximum(m, jnp.max(x, 0))
 
-    def weights(b, mc, l):
+    def weights(b, mc, l, sbuf, pbuf):
         p = jnp.exp2(sbuf[pl.ds(b * BLOCK, BLOCK), :] * c2 - mc)
         pbuf[:, pl.ds(b * BLOCK, BLOCK)] = p.astype(jnp.bfloat16).T
         return l + jnp.sum(p.reshape(BLOCK // heads, heads, 2 * nq), 0)
 
-    def values(s, b, acc):
+    def values(s, b, acc, pbuf):
         slot = lax.rem(s, SLOTS)
         at = pl.ds(b * BLOCK, BLOCK)
         acc = acc + jnp.dot(pbuf[:nq, at], vbuf[slot, at, :], preferred_element_type=jnp.float32)
@@ -81,7 +84,10 @@
         x = reduce(x, 0, keepdims=True)
         return op(x, pltpu.roll(x, nq, 1))
 
-    def stage(s, state, which):
+    def stat_of(m, l):
+        return jnp.where(first, m, fold(l, jnp.add, jnp.sum))
+
+    def stage(s, side, state, which):
         m8, l8, m2 = state
         m = jnp.full((heads, 2 * nq), -jnp.inf, jnp.float32)
         l = jnp.zeros((heads, 2 * nq), jnp.float32)
@@ -93,14 +99,15 @@
         m1 = fold(m8, jnp.maximum, jnp.max)
         for b in range(nblk):
             if "C" in which:
-                acc = values(s - 2, b, acc)
+                acc = values(s - 2, b, acc, pbufs[side])
             if "B" in which:
-                l = weights(b, m1 * c2, l)
+                l = weights(b, m1 * c2, l, sbufs[1 - side], pbufs[1 - side])
             if "A" in which:
-                m = scores(s, b, w, m)
+                m = scores(s, b, w, m, sbufs[side])
         if "C" in which:
             send[pl.ds((s - 2) * per, per)] = acc.reshape(per, SUB, d).astype(send.dtype)
-            stat[s - 2] = jnp.where(first, m2, fold(l8, jnp.add, jnp.sum))
+            if "B" in which:
+                stat[s - 2] = stat_of(m2, l8)
         return m, l, m1
 
     def shape_of(c):
@@ -122,12 +129,23 @@
     def wait_for(ref, sem):
         pltpu.make_async_copy(ref, ref, sem).wait()
 
+    def peers():
+        for i in [x for k in range(zs // 2) for x in (zs // 2 - k, zs // 2 + k)[: 1 + (k > 0)]]:
+            for k in range(CORES):
+                yield lax.rem(z + i, zs) * CORES + lax.rem(core + k, CORES)
+        for k in range(1, CORES):
+            yield z * CORES + lax.rem(core + k, CORES)
+
+    def send_part(c, j):
+        remote(send.at[rows_of(c, owner(j))], recv[c].at[me], sems.at[PART_OUT, c], sems.at[PART_IN, c], j).start()
+
+    def send_stat(c, j):
+        remote(stat.at[seq_of(c, owner(j))], rstat[c].at[me], sems.at[STAT_OUT, c], sems.at[STAT_IN, c], j).start()
+
     def send_parts(c):
-        for i in range(1, size):
-            j = lax.rem(me + i, size)
-            o = owner(j)
-            remote(send.at[rows_of(c, o)], recv[c].at[me], sems.at[PART_OUT, c], sems.at[PART_IN, c], j).start()
-            remote(stat.at[seq_of(c, o)], rstat[c].at[me], sems.at[STAT_OUT, c], sems.at[STAT_IN, c], j).start()
+        for j in peers():
+            send_part(c, j)
+            send_stat(c, j)
 
     def combine(c, direct):
         base, g, r = shape_of(c)
@@ -146,12 +164,9 @@
             acc = acc + recv[c][j].astype(jnp.float32).reshape(r * SUB, d) * f[:, j : j + 1]
         mine = rows_of(c, o)
         o_ref[mine] = acc.reshape(r, SUB, d).astype(o_ref.dtype)
-        if direct:
-            peers = [lax.rem(me + i, size) for i in range(1, size)]
-        else:
-            peers = [lax.rem(z + i, zs) * CORES + core for i in range(1, zs)]
-        for j in peers:
-            remote(o_ref.at[mine], o_ref.at[mine], sems.at[RES_OUT, c], sems.at[RES_IN, c], j).start()
+        for i, j in enumerate(peers()):
+            if direct or i % CORES == 0 and i < (zs - 1) * CORES:
+                remote(o_ref.at[mine], o_ref.at[mine], sems.at[RES_OUT, c], sems.at[RES_IN, c], j).start()
 
     def count(c, k):
         return o_ref.at[pl.ds(0, k * shape_of(c)[2])]
@@ -165,7 +180,7 @@
     last = nc - 1
     ends = [base + g for base, g in chunks]
     events = {}
-    for c in range(nc):
+    for c in range(last):
         events.setdefault(ends[c], []).append(functools.partial(send_parts, c))
     late = []
     for c in range(last):
@@ -183,40 +198,56 @@
         def _():
             copy(s + SLOTS).start()
 
+    qcopy.wait()
     kcopy(0).wait()
-    state = stage(0, state, "A")
+    state = stage(0, 0, state, "A")
     refill(kcopy, 0)
     kcopy(1).wait()
-    state = stage(1, state, "BA")
+    state = stage(1, 1, state, "BA")
     refill(kcopy, 1)
 
-    def body(s, state):
-        kcopy(s).wait()
-        vcopy(s - 2).wait()
-        state = stage(s, state, "ABC")
-        refill(kcopy, s)
-        refill(vcopy, s - 2)
+    def body(i, state):
+        s = 2 * i
+        for u in range(2):
+            kcopy(s + u).wait()
+            vcopy(s + u - 2).wait()
+        for u in range(2):
+            state = stage(s + u, u, state, "ABC")
+        for u in range(2):
+            refill(kcopy, s + u)
+            refill(vcopy, s + u - 2)
         return state
 
     at = 2
     waited = False
-    for e in sorted(x for x in events if x <= n - 2) + [n - 2]:
-        if e + 2 > at:
-            state = lax.fori_loop(at, e + 2, body, state)
-            at = e + 2
+    for e in sorted(x for x in events if x <= n - 2):
+        state = lax.fori_loop(at // 2, e // 2 + 1, body, state)
+        at = e + 2
         if not waited:
             pl.semaphore_wait(barrier, size - 1)
             waited = True
-        for run in events.pop(e, []):
+        for run in events.pop(e):
             run()
+    assert at == n
     vcopy(n - 2).wait()
-    state = stage(n, state, "BC")
-    for run in events.pop(n - 1, []):
-        run()
+    m8, l8, m2 = stage(n, 0, state, "BC")
+    stat[n - 1] = stat_of(m2, l8)
+    for j in peers():
+        send_stat(last, j)
+    for i in range(zs):
+        if i:
+            send_part(last, lax.rem(z + i, zs) * CORES)
+    @pl.when(core != 0)
+    def _():
+        send_part(last, z * CORES)
     vcopy(n - 1).wait()
-    state = stage(n + 1, state, "C")
-    for run in events.pop(n, []):
-        run()
+    stage(n + 1, 1, (m8, l8, m2), "C")
+    for i in range(zs):
+        if i:
+            send_part(last, lax.rem(z + i, zs) * CORES + 1)
+    @pl.when(core == 0)
+    def _():
+        send_part(last, z * CORES + 1)
     for c in early:
         pass_on(c)
     for c in late:
@@ -248,19 +279,21 @@
         rows = t * heads
         out = pl.pallas_call(
             functools.partial(kernel, size, chunks, d**-0.5, heads),
-            out_shape=jax.ShapeDtypeStruct((n * per, SUB, d), q.dtype),
-            in_specs=[pl.BlockSpec(memory_space=pltpu.VMEM), pl.BlockSpec(memory_space=pl.ANY), pl.BlockSpec(memory_space=pl.ANY)],
+            out_shape=pltpu.VMEM((n * per, SUB, d), q.dtype),
+            in_specs=[pl.BlockSpec(memory_space=pl.ANY)] * 3,
             out_specs=pl.BlockSpec(memory_space=pltpu.VMEM),
             scratch_shapes=[
+                pltpu.VMEM(q.shape, q.dtype),
                 pltpu.VMEM((SLOTS, rows, d), k.dtype),
                 pltpu.VMEM((SLOTS, rows, d), v.dtype),
-                pltpu.VMEM((rows // 2, 2 * nq), jnp.float32),
-                pltpu.VMEM((2 * nq, rows // 2), jnp.bfloat16),
+                *[pltpu.VMEM((rows // 2, 2 * nq), jnp.float32)] * 2,
+                *[pltpu.VMEM((2 * nq, rows // 2), jnp.bfloat16)] * 2,
                 pltpu.VMEM((n * per, SUB, d), jnp.bfloat16),
                 pltpu.VMEM((n, 1, 2 * nq), jnp.float32),
                 pltpu.VMEM((2 * nq, size), jnp.float32),
                 *[pltpu.VMEM((size, g * per // size, SUB, d), jnp.bfloat16) for _, g in chunks],
                 *[pltpu.VMEM((size, 1, 2 * nq), jnp.float32) for _ in chunks],
+                pltpu.SemaphoreType.DMA,
                 pltpu.SemaphoreType.DMA((SLOTS,)),
                 pltpu.SemaphoreType.DMA((SLOTS,)),
                 pltpu.SemaphoreType.DMA((8, nc)),

time: 48.7 us -> 48.4 us (level)
  local copies, waits for them, and re-layouts: 1.87 us -> 0.8 us
  Pallas kernels: 46.7 us -> 47.5 us
    unnamed x1, local copies, waits for them, and re-layouts: 1.87 us -> 0.8 us
    pallas_call x1, Pallas kernels: 46.7 us -> 47.5 us  [step(): pl.pallas_call(functools.partial(kernel, size, chunks, d ** (-0.5), heads...]
where the time goes in v2:
time: 48.4 us; the launch traced here: 48.3 us
  Pallas kernels  47.5 us (98%)
  local copies, waits for them, and re-layouts  0.8 us (2%)
    pallas_call x1, Pallas kernels, step(): pl.pallas_call(functools.partial(kernel, size, chunks, d ** (-0.5), heads...  47.5 us

profile of v2, /device:TPU:21, one launch (start us, length us, event | category | flops | bytes accessed | tf_op | source)
XLA Modules:
  0.0 48.3 jit_solution(1998606574490107156)
XLA Ops:
  0.0 47.5 %shard_map.37 = bf16[256,8,128]{2,1,0:T(8,128)(2,1)S(1)} custom-call(bf16[32,64,128]{2,1,0:T(8,128)(2,1)} %q_hbm.1, bf16[32,4096,128]{2,1,0:T(8,128)(2,1)} %bitcast.4, bf16[32,4096,128]{2,1,0:T(8,128)(2,1)} %bitcast.5), custom_call_target="tpu_custom_call" | custom-call | tf_op jit(solution)/shard_map/pallas_call | solution.py:280
  47.5 0.8 %copy.5 = bf16[32,64,128]{2,1,0:T(8,128)(2,1)} copy(bf16[32,64,128]{2,1,0:T(8,128)(2,1)S(1)} %bitcast.3) | data formatting | bytes 1048576

commit v3 on v2

--- a/solution.py
+++ b/solution.py
@@ -10,12 +10,13 @@
 SLOTS = 8
 BLOCK = 512
 CORES = 2
+JOIN_LAG = 10
 SUB = 8
 LOG2E = 1.4426950408889634
 
 
 def chunks_of(n, unit):
-    sizes = [4 * unit] * (n // (4 * unit) - 1) + [2 * unit, unit, unit]
+    sizes = [8 * unit, 4 * unit, 2 * unit, 2 * unit]
     assert sum(sizes) == n
     return [(sum(sizes[:i]), g) for i, g in enumerate(sizes)]
 
@@ -36,8 +37,14 @@
     zs = size // CORES
     core, z = lax.rem(me, CORES), me // CORES
 
+    def spread(z):
+        return lax.rem(z * (zs // 2 + 1), zs)
+
     def owner(j):
-        return lax.rem(j, CORES) * zs + j // CORES
+        return lax.rem(j, CORES) * zs + spread(j // CORES)
+
+    def device(o):
+        return spread(lax.rem(o, zs)) * CORES + o // zs
 
     barrier = pltpu.get_barrier_semaphore()
     for i in range(1, size):
@@ -136,16 +143,20 @@
         for k in range(1, CORES):
             yield z * CORES + lax.rem(core + k, CORES)
 
-    def send_part(c, j):
-        remote(send.at[rows_of(c, owner(j))], recv[c].at[me], sems.at[PART_OUT, c], sems.at[PART_IN, c], j).start()
-
-    def send_stat(c, j):
-        remote(stat.at[seq_of(c, owner(j))], rstat[c].at[me], sems.at[STAT_OUT, c], sems.at[STAT_IN, c], j).start()
-
-    def send_parts(c):
-        for j in peers():
-            send_part(c, j)
-            send_stat(c, j)
+    def owners_of(c, s):
+        base, _, r = shape_of(c)
+        return [(s - base) * (per // r) + i for i in range(per // r)]
+
+    def to_owners(c, s, part=True, stats=True):
+        for o in owners_of(c, s):
+            j = device(o)
+
+            @pl.when(j != me)
+            def _():
+                if stats:
+                    remote(stat.at[s], rstat[c].at[me], sems.at[STAT_OUT, c], sems.at[STAT_IN, c], j).start()
+                if part:
+                    remote(send.at[rows_of(c, o)], recv[c].at[me], sems.at[PART_OUT, c], sems.at[PART_IN, c], j).start()
 
     def combine(c, direct):
         base, g, r = shape_of(c)
@@ -178,18 +189,7 @@
         remote(own, own, sems.at[PASS_OUT, c], sems.at[PASS_IN, c], z * CORES + lax.rem(core + 1, CORES)).start()
 
     last = nc - 1
-    ends = [base + g for base, g in chunks]
-    events = {}
-    for c in range(last):
-        events.setdefault(ends[c], []).append(functools.partial(send_parts, c))
-    late = []
-    for c in range(last):
-        at = ends[c] + chunks[c][1] + chunks[c][1] // 2
-        if at < n - 1:
-            events.setdefault(at, []).append(functools.partial(combine, c, False))
-        else:
-            late.append(c)
-    early = [c for c in range(last) if c not in late]
+    joined = JOIN_LAG + chunks[0][1]
 
     state = (jnp.zeros((heads, 2 * nq), jnp.float32), jnp.zeros((heads, 2 * nq), jnp.float32), jnp.zeros((1, 2 * nq), jnp.float32))
 
@@ -206,7 +206,7 @@
     state = stage(1, 1, state, "BA")
     refill(kcopy, 1)
 
-    def body(i, state):
+    def body(c, i, state):
         s = 2 * i
         for u in range(2):
             kcopy(s + u).wait()
@@ -216,44 +216,30 @@
         for u in range(2):
             refill(kcopy, s + u)
             refill(vcopy, s + u - 2)
+        for u in range(2):
+            to_owners(c, s + u - 2)
         return state
 
-    at = 2
-    waited = False
-    for e in sorted(x for x in events if x <= n - 2):
-        state = lax.fori_loop(at // 2, e // 2 + 1, body, state)
-        at = e + 2
-        if not waited:
-            pl.semaphore_wait(barrier, size - 1)
-            waited = True
-        for run in events.pop(e):
-            run()
-    assert at == n
+    pl.semaphore_wait(barrier, size - 1)
+    for c, (base, g) in enumerate(chunks):
+        for lo, hi in ((base, min(base + g, joined)), (max(base, joined), min(base + g, n - 2))):
+            if lo < hi:
+                state = lax.fori_loop(lo // 2 + 1, hi // 2 + 1, functools.partial(body, c), state)
+                if hi == joined:
+                    combine(0, False)
     vcopy(n - 2).wait()
     m8, l8, m2 = stage(n, 0, state, "BC")
     stat[n - 1] = stat_of(m2, l8)
-    for j in peers():
-        send_stat(last, j)
-    for i in range(zs):
-        if i:
-            send_part(last, lax.rem(z + i, zs) * CORES)
-    @pl.when(core != 0)
-    def _():
-        send_part(last, z * CORES)
+    to_owners(last, n - 2)
+    to_owners(last, n - 1, part=False)
     vcopy(n - 1).wait()
     stage(n + 1, 1, (m8, l8, m2), "C")
-    for i in range(zs):
-        if i:
-            send_part(last, lax.rem(z + i, zs) * CORES + 1)
-    @pl.when(core == 0)
-    def _():
-        send_part(last, z * CORES + 1)
-    for c in early:
-        pass_on(c)
-    for c in late:
+    to_owners(last, n - 1, stats=False)
+    for c in range(1, last):
         combine(c, False)
+    pass_on(0)
     combine(last, True)
-    for c in late:
+    for c in range(1, last):
         pass_on(c)
     for c in range(last):
         base, g, r = shape_of(c)

time: 48.4 us -> 44.1 us (0.911)
  Pallas kernels: 47.5 us -> 43.3 us
    pallas_call x1, Pallas kernels: 47.5 us -> 43.3 us  [step(): pl.pallas_call(functools.partial(kernel, size, chunks, d ** (-0.5), heads...]
where the time goes in v3:
time: 44.1 us
  Pallas kernels  43.3 us (98%)
  local copies, waits for them, and re-layouts  0.8 us (2%)
    pallas_call x1, Pallas kernels, step(): pl.pallas_call(functools.partial(kernel, size, chunks, d ** (-0.5), heads...  43.3 us

profile of v3, /device:TPU:21, one launch (start us, length us, event | category | flops | bytes accessed | tf_op | source)
XLA Modules:
  0.0 44.1 jit_solution(5773820181056597586)
XLA Ops:
  0.0 43.3 %shard_map.37 = bf16[256,8,128]{2,1,0:T(8,128)(2,1)S(1)} custom-call(bf16[32,64,128]{2,1,0:T(8,128)(2,1)} %q_hbm.1, bf16[32,4096,128]{2,1,0:T(8,128)(2,1)} %bitcast.4, bf16[32,4096,128]{2,1,0:T(8,128)(2,1)} %bitcast.5), custom_call_target="tpu_custom_call" | custom-call | tf_op jit(solution)/shard_map/pallas_call | solution.py:266
  43.3 0.8 %copy.5 = bf16[32,64,128]{2,1,0:T(8,128)(2,1)} copy(bf16[32,64,128]{2,1,0:T(8,128)(2,1)S(1)} %bitcast.3) | data formatting | bytes 1048576

commit v4 on v3

--- a/solution.py
+++ b/solution.py
@@ -161,15 +161,15 @@
     def combine(c, direct):
         base, g, r = shape_of(c)
         o = owner(me)
-        recv[c][me] = send[rows_of(c, o)]
         rstat[c][me] = stat[seq_of(c, o)]
         wait_for(rstat[c].at[pl.ds(0, size - 1)], sems.at[STAT_IN, c])
-        wait_for(recv[c].at[pl.ds(0, size - 1)], sems.at[PART_IN, c])
         st = rstat[c][...].reshape(size, 2 * nq)
         e = jnp.exp2((st - jnp.max(st, 0, keepdims=True)) * c2)
         f = e / jnp.sum(e * pltpu.roll(st, nq, 1), 0, keepdims=True)
         cols[...] = f.T
         f = cols[pl.ds(pl.multiple_of(lax.rem(o * r, per) * SUB, SUB), r * SUB), :]
+        recv[c][me] = send[rows_of(c, o)]
+        wait_for(recv[c].at[pl.ds(0, size - 1)], sems.at[PART_IN, c])
         acc = jnp.zeros((r * SUB, d), jnp.float32)
         for j in range(size):
             acc = acc + recv[c][j].astype(jnp.float32).reshape(r * SUB, d) * f[:, j : j + 1]
@@ -189,7 +189,7 @@
         remote(own, own, sems.at[PASS_OUT, c], sems.at[PASS_IN, c], z * CORES + lax.rem(core + 1, CORES)).start()
 
     last = nc - 1
-    joined = JOIN_LAG + chunks[0][1]
+    assert chunks[0][1] == size and size + JOIN_LAG <= n - 4
 
     state = (jnp.zeros((heads, 2 * nq), jnp.float32), jnp.zeros((heads, 2 * nq), jnp.float32), jnp.zeros((1, 2 * nq), jnp.float32))
 
@@ -218,15 +218,23 @@
             refill(vcopy, s + u - 2)
         for u in range(2):
             to_owners(c, s + u - 2)
+
+        @pl.when(owner(me) // 2 == i - 1 - JOIN_LAG // 2)
+        def _():
+            combine(0, False)
+
         return state
 
     pl.semaphore_wait(barrier, size - 1)
     for c, (base, g) in enumerate(chunks):
-        for lo, hi in ((base, min(base + g, joined)), (max(base, joined), min(base + g, n - 2))):
-            if lo < hi:
-                state = lax.fori_loop(lo // 2 + 1, hi // 2 + 1, functools.partial(body, c), state)
-                if hi == joined:
-                    combine(0, False)
+        lo, hi = base, min(base + g, n - 4)
+        if lo < hi:
+            state = lax.fori_loop(lo // 2 + 1, hi // 2 + 1, functools.partial(body, c), state)
+    for s in (n - 2, n - 1):
+        kcopy(s).wait()
+        vcopy(s - 2).wait()
+        state = stage(s, s % 2, state, "ABC")
+        to_owners(last, s - 2)
     vcopy(n - 2).wait()
     m8, l8, m2 = stage(n, 0, state, "BC")
     stat[n - 1] = stat_of(m2, l8)

time: 44.1 us -> 43.1 us (0.977)
  Pallas kernels: 43.3 us -> 42.2 us
    pallas_call x1, Pallas kernels: 43.3 us -> 42.2 us  [step(): pl.pallas_call(functools.partial(kernel, size, chunks, d ** (-0.5), heads...]
where the time goes in v4:
time: 43.1 us
  Pallas kernels  42.2 us (98%)
  local copies, waits for them, and re-layouts  0.8 us (2%)
    pallas_call x1, Pallas kernels, step(): pl.pallas_call(functools.partial(kernel, size, chunks, d ** (-0.5), heads...  42.2 us

profile of v4, /device:TPU:21, one launch (start us, length us, event | category | flops | bytes accessed | tf_op | source)
XLA Modules:
  0.0 43.1 jit_solution(17983894510758512108)
XLA Ops:
  0.0 42.2 %shard_map.37 = bf16[256,8,128]{2,1,0:T(8,128)(2,1)S(1)} custom-call(bf16[32,64,128]{2,1,0:T(8,128)(2,1)} %q_hbm.1, bf16[32,4096,128]{2,1,0:T(8,128)(2,1)} %bitcast.4, bf16[32,4096,128]{2,1,0:T(8,128)(2,1)} %bitcast.5), custom_call_target="tpu_custom_call" | custom-call | tf_op jit(solution)/shard_map/pallas_call | solution.py:274
  42.3 0.8 %copy.5 = bf16[32,64,128]{2,1,0:T(8,128)(2,1)} copy(bf16[32,64,128]{2,1,0:T(8,128)(2,1)S(1)} %bitcast.3) | data formatting | bytes 1048576

commit v5 on v4

--- a/solution.py
+++ b/solution.py
@@ -7,16 +7,17 @@
 from jax.experimental.pallas import tpu as pltpu
 from jax.sharding import PartitionSpec as P
 
+EARLY = 3
 SLOTS = 8
 BLOCK = 512
 CORES = 2
-JOIN_LAG = 10
+JOIN_LAG = 12
 SUB = 8
 LOG2E = 1.4426950408889634
 
 
 def chunks_of(n, unit):
-    sizes = [8 * unit, 4 * unit, 2 * unit, 2 * unit]
+    sizes = [8 * unit, 4 * unit, 4 * unit]
     assert sum(sizes) == n
     return [(sum(sizes[:i]), g) for i, g in enumerate(sizes)]
 
@@ -58,7 +59,7 @@
 
     qcopy = pltpu.make_async_copy(q_hbm, q_ref, qsem)
     qcopy.start()
-    for s in range(SLOTS):
+    for s in range(EARLY):
         kcopy(s).start()
         vcopy(s).start()
 
@@ -200,6 +201,9 @@
 
     qcopy.wait()
     kcopy(0).wait()
+    for s in range(EARLY, SLOTS):
+        kcopy(s).start()
+        vcopy(s).start()
     state = stage(0, 0, state, "A")
     refill(kcopy, 0)
     kcopy(1).wait()

time: 43.1 us -> 40.8 us (0.947)
  Pallas kernels: 42.2 us -> 39.9 us
    pallas_call x1, Pallas kernels: 42.2 us -> 39.9 us  [step(): pl.pallas_call(functools.partial(kernel, size, chunks, d ** (-0.5), heads...]
where the time goes in v5:
time: 40.8 us; the launch traced here: 40.7 us
  Pallas kernels  39.9 us (98%)
  local copies, waits for them, and re-layouts  0.8 us (2%)
    pallas_call x1, Pallas kernels, step(): pl.pallas_call(functools.partial(kernel, size, chunks, d ** (-0.5), heads...  39.9 us

profile of v5, /device:TPU:21, one launch (start us, length us, event | category | flops | bytes accessed | tf_op | source)
XLA Modules:
  0.0 40.7 jit_solution(15932820494137812151)
XLA Ops:
  0.0 39.9 %shard_map.37 = bf16[256,8,128]{2,1,0:T(8,128)(2,1)S(1)} custom-call(bf16[32,64,128]{2,1,0:T(8,128)(2,1)} %q_hbm.1, bf16[32,4096,128]{2,1,0:T(8,128)(2,1)} %bitcast.4, bf16[32,4096,128]{2,1,0:T(8,128)(2,1)} %bitcast.5), custom_call_target="tpu_custom_call" | custom-call | tf_op jit(solution)/shard_map/pallas_call | solution.py:278
  39.9 0.8 %copy.5 = bf16[32,64,128]{2,1,0:T(8,128)(2,1)} copy(bf16[32,64,128]{2,1,0:T(8,128)(2,1)S(1)} %bitcast.3) | data formatting | bytes 1048576
